TPU v7x, 32 devices: a whole 2x2x4 slice. The times are simulated.
32 devices in a mesh: dp: 8 (over y, x, core), tensor: 4 (over z).
Axes of the slice: x: 2, y: 2, z: 4, core: 2. Of those that a mesh axis runs over, the one named last changes fastest.
Arguments:
- tokens: bfloat16 [8192, 1536], P(('dp', 'tensor')), may hold values from -6 to 6
- segments: int32 [8, 1024], P('dp'), may hold values from 0 to 3, never falling along the last dimension, each value on 1 to 512 neighbouring positions
- gain_one: bfloat16 [1536], P('dp'), may hold values from 0.25 to 1.75
- query_w: bfloat16 [1536, 1536], P('dp', 'tensor'), may hold values from -0.15625 to 0.15625
- query_b: bfloat16 [1536], P('tensor'), may hold values from -3 to 3
- key_w: bfloat16 [1536, 256], P('dp'), may hold values from -0.15625 to 0.15625
- key_b: bfloat16 [256], replicated, may hold values from -3 to 3
- value_w: bfloat16 [1536, 256], P('dp'), may hold values from -0.15625 to 0.15625
- value_b: bfloat16 [256], replicated, may hold values from -3 to 3
- out_w: bfloat16 [1536, 1536], P('dp', 'tensor'), may hold values from -0.4375 to 0.4375
- gain_two: bfloat16 [1536], P('dp'), may hold values from 0.25 to 1.75
- gate_w: bfloat16 [1536, 8960], P('dp', 'tensor'), may hold values from -0.15625 to 0.15625
- up_w: bfloat16 [1536, 8960], P('dp', 'tensor'), may hold values from -0.15625 to 0.15625
- down_w: bfloat16 [1536, 8960], P('dp', 'tensor'), may hold values from -0.0625 to 0.0625
- cotangent: bfloat16 [8192, 1536], P(('dp', 'tensor')), may hold values from -6 to 6
Outputs:
- mixed: bfloat16 [8192, 1536], P(('dp', 'tensor'))
- input_grad: bfloat16 [8192, 1536], P(('dp', 'tensor'))
- grad_gain_one: float32 [1536], P(('dp', 'tensor'))
- grad_query_w: float32 [1536, 1536], P('dp', 'tensor')
- grad_query_b: float32 [1536], P(('dp', 'tensor'))
- grad_key_w: float32 [1536, 256], P(('dp', 'tensor'))
- grad_key_b: float32 [256], replicated
- grad_value_w: float32 [1536, 256], P(('dp', 'tensor'))
- grad_value_b: float32 [256], replicated
- grad_out_w: float32 [1536, 1536], P('dp', 'tensor')
- grad_gain_two: float32 [1536], P(('dp', 'tensor'))
- grad_gate_w: float32 [1536, 8960], P('dp', 'tensor')
- grad_up_w: float32 [1536, 8960], P('dp', 'tensor')
- grad_down_w: float32 [1536, 8960], P('dp', 'tensor')
Inputs may be any that keep to these rules, and one draw needn't show every extreme that they name: `segments`: in each sequence of 1024 positions the document numbers never fall; each of the 4 documents covers 1 to 512 positions, and one covers exactly 512.
All inputs are finite; a program needn't handle non-finite values.
Results may differ from a plain program's by a relative error of at most 0.02.
Values may be sent and summed in bfloat16 or wider, within the bound.
A program may use at most 256 MiB of HBM per device.

v0:
```python
import jax
import jax.numpy as jnp
from jax import lax
from jax.sharding import PartitionSpec as P

KV_HEADS = 2
HEAD_DIM = 128
DOC_MAX = 512
EPSILON = 1e-06
ROPE_BASE = 1000000.0
NEGATIVE = -1e30


def angle_tables(first, length, head_width):
    position = (first + jnp.arange(length)).astype(jnp.float32)
    exponent = jnp.arange(head_width // 2, dtype=jnp.float32) * (2.0 / head_width)
    frequency = ROPE_BASE ** (-exponent)
    angle = position[:, None] * frequency[None, :]
    return (jnp.cos(angle), jnp.sin(angle))


def rotate(values, cosine, sine):
    half_width = values.shape[-1] // 2
    first_half = values[..., :half_width]
    second_half = values[..., half_width:]
    return jnp.concatenate(
        [first_half * cosine - second_half * sine, second_half * cosine + first_half * sine],
        axis=-1,
    )


def rotate_back(grads, cosine, sine):
    return rotate(grads, cosine, -sine)


def dot_f32(left, right, dims):
    return lax.dot_general(left, right, (dims, ((), ())), preferred_element_type=jnp.float32)


def contract_rows(left, right):
    return dot_f32(left, right, ((0,), (0,)))


def contract_cols(left, right):
    return dot_f32(left, right, ((1,), (1,)))


def norm_back(upstream, unit, inverse, gain):
    scaled = upstream * gain
    gain_term = jnp.sum(upstream * unit, axis=0)
    input_term = inverse * (scaled - unit * jnp.mean(scaled * unit, axis=-1, keepdims=True))
    return (gain_term, input_term)


def local(
    tokens,
    segments,
    gain_one,
    query_w,
    query_b,
    key_w,
    key_b,
    value_w,
    value_b,
    out_w,
    gain_two,
    gate_w,
    up_w,
    down_w,
    cotangent,
):
    bf16, f32 = (jnp.bfloat16, jnp.float32)
    model_width = tokens.shape[1]
    rows = tokens.shape[0]
    tensor_size = lax.axis_size("tensor")
    rank = lax.axis_index("tensor")
    seq_length = rows * tensor_size
    kv_width = key_w.shape[1]
    query_width = query_w.shape[1] * tensor_size
    heads = query_width // HEAD_DIM
    group = heads // KV_HEADS
    scale = HEAD_DIM ** (-0.5)
    pair = lax.all_gather(jnp.stack([query_w, out_w]), "tensor", axis=2, tiled=True)
    joined = jnp.concatenate([pair[0], key_w, value_w, pair[1]], axis=1)
    joined = lax.all_gather(joined, "dp", axis=0, tiled=True)
    qkv_width = query_width + 2 * kv_width
    qkv_w = joined[:, :qkv_width]
    out_full = joined[:, qkv_width:]
    gains = lax.all_gather(jnp.stack([gain_one, gain_two]), "dp", axis=1, tiled=True).astype(f32)
    full_query_b = lax.all_gather(query_b, "tensor", axis=0, tiled=True)
    qkv_b = jnp.concatenate([full_query_b, key_b, value_b]).astype(f32)
    full_gate = lax.all_gather(gate_w, "dp", axis=0, tiled=True)
    full_up = lax.all_gather(up_w, "dp", axis=0, tiled=True)
    full_down = lax.all_gather(down_w, "dp", axis=0, tiled=True)
    cot_rows = lax.all_gather(cotangent, "tensor", axis=0, tiled=True)
    inputs = tokens.astype(f32)
    inverse_one = lax.rsqrt(jnp.mean(inputs * inputs, axis=-1, keepdims=True) + EPSILON)
    unit_one = inputs * inverse_one
    normed_one = (unit_one * gains[0]).astype(bf16)
    lin = jnp.dot(normed_one, qkv_w, preferred_element_type=f32) + qkv_b
    cosine, sine = angle_tables(rank * rows, rows, HEAD_DIM)
    cos_h, sin_h = (cosine[:, None, :], sine[:, None, :])
    query_rot = rotate(lin[:, :query_width].reshape(rows, heads, HEAD_DIM), cos_h, sin_h).astype(
        bf16
    )
    key_rot = rotate(
        lin[:, query_width : query_width + kv_width].reshape(rows, KV_HEADS, HEAD_DIM), cos_h, sin_h
    ).astype(bf16)
    value_own = lin[:, query_width + kv_width :].astype(bf16)
    kv_own = jnp.concatenate([key_rot.reshape(rows, kv_width), value_own], axis=1)
    kv_all = lax.all_gather(kv_own, "tensor", axis=0, tiled=True)
    window = min(seq_length, rows + -(-DOC_MAX // rows) * rows)
    first = jnp.maximum((rank + 1) * rows - window, 0)
    kv_win = lax.dynamic_slice_in_dim(kv_all, first, window, 0)
    key_win = kv_win[:, :kv_width].reshape(window, KV_HEADS, HEAD_DIM)
    value_win = kv_win[:, kv_width:].reshape(window, KV_HEADS, HEAD_DIM)
    segment = segments[0]
    own_segment = lax.dynamic_slice_in_dim(segment, rank * rows, rows, 0)
    win_segment = lax.dynamic_slice_in_dim(segment, first, window, 0)
    own_pos = rank * rows + jnp.arange(rows)
    win_pos = first + jnp.arange(window)
    allowed = (own_segment[:, None] == win_segment[None, :]) & (
        win_pos[None, :] <= own_pos[:, None]
    )
    grouped = query_rot.reshape(rows, KV_HEADS, group, HEAD_DIM)
    scores = jnp.einsum("tagd,sad->agts", grouped, key_win, preferred_element_type=f32) * scale
    masked = jnp.where(allowed, scores, NEGATIVE)
    largest = jnp.max(masked, axis=-1, keepdims=True)
    log_total = largest + jnp.log(jnp.sum(jnp.exp(masked - largest), axis=-1, keepdims=True))
    probs = jnp.exp(masked - log_total)
    probs_low = probs.astype(bf16)
    context = jnp.einsum("agts,sad->tagd", probs_low, value_win, preferred_element_type=f32)
    context = context.reshape(rows, query_width).astype(bf16)
    middle = inputs + contract_cols(context, out_full)
    inverse_two = lax.rsqrt(jnp.mean(middle * middle, axis=-1, keepdims=True) + EPSILON)
    unit_two = middle * inverse_two
    normed_two = (unit_two * gains[1]).astype(bf16)
    rows_two = lax.all_gather(normed_two, "tensor", axis=0, tiled=True)
    gate = jnp.dot(rows_two, full_gate, preferred_element_type=f32)
    upper = jnp.dot(rows_two, full_up, preferred_element_type=f32)
    sigmoid = jax.nn.sigmoid(gate)
    hidden_low = (gate * sigmoid * upper).astype(bf16)
    ffn_sum = lax.psum_scatter(
        contract_cols(hidden_low, full_down).astype(bf16), "tensor", scatter_dimension=0, tiled=True
    ).astype(f32)
    mixed = (middle + ffn_sum).astype(bf16)
    d_hidden = jnp.dot(cot_rows, full_down, preferred_element_type=f32)
    d_upper = (d_hidden * gate * sigmoid).astype(bf16)
    d_gate = (d_hidden * upper * sigmoid * (1.0 + gate * (1.0 - sigmoid))).astype(bf16)
    d_normed_two = lax.psum_scatter(
        (contract_cols(d_gate, full_gate) + contract_cols(d_upper, full_up)).astype(bf16),
        "tensor",
        scatter_dimension=0,
        tiled=True,
    ).astype(f32)
    grad_down = contract_rows(cot_rows, hidden_low).astype(bf16)
    grad_gate = contract_rows(rows_two, d_gate).astype(bf16)
    grad_up = contract_rows(rows_two, d_upper).astype(bf16)
    gain_two_term, d_from_two = norm_back(d_normed_two, unit_two, inverse_two, gains[1])
    d_middle = cotangent.astype(f32) + d_from_two
    d_attended = d_middle.astype(bf16)
    d_context = jnp.dot(d_attended, out_full, preferred_element_type=f32).astype(bf16)
    grad_out = contract_rows(d_attended, context).astype(bf16)
    d_context = d_context.reshape(rows, KV_HEADS, group, HEAD_DIM)
    d_probs = jnp.einsum("tagd,sad->agts", d_context, value_win, preferred_element_type=f32)
    row_delta = jnp.sum(probs * d_probs, axis=-1, keepdims=True)
    d_scores = (probs * (d_probs - row_delta)).astype(bf16)
    d_query_rot = (
        jnp.einsum("agts,sad->tagd", d_scores, key_win, preferred_element_type=f32) * scale
    )
    d_key_win = jnp.einsum("agts,tagd->sad", d_scores, grouped, preferred_element_type=f32) * scale
    d_value_win = jnp.einsum("agts,tagd->sad", probs_low, d_context, preferred_element_type=f32)
    d_query_lin = (
        rotate_back(d_query_rot.reshape(rows, heads, HEAD_DIM), cos_h, sin_h)
        .reshape(rows, query_width)
        .astype(bf16)
    )
    d_kv_win = jnp.concatenate(
        [d_key_win.reshape(window, kv_width), d_value_win.reshape(window, kv_width)], axis=1
    ).astype(bf16)
    d_kv_all = lax.dynamic_update_slice(
        jnp.zeros((seq_length, 2 * kv_width), bf16), d_kv_win, (first, 0)
    )
    d_kv = lax.psum_scatter(d_kv_all, "tensor", scatter_dimension=0, tiled=True).astype(f32)
    d_key_lin = rotate_back(d_kv[:, :kv_width].reshape(rows, KV_HEADS, HEAD_DIM), cos_h, sin_h)
    d_lin = jnp.concatenate(
        [
            d_query_lin,
            d_key_lin.reshape(rows, kv_width).astype(bf16),
            d_kv[:, kv_width:].astype(bf16),
        ],
        axis=1,
    )
    d_normed_one = contract_cols(d_lin, qkv_w)
    grad_qkv = contract_rows(normed_one, d_lin).astype(bf16)
    bias_term = jnp.sum(d_lin.astype(f32), axis=0)
    gain_one_term, d_from_one = norm_back(d_normed_one, unit_one, inverse_one, gains[0])
    input_grad = (d_middle + d_from_one).astype(bf16)

    def over_dp(grad):
        return lax.psum_scatter(grad, "dp", scatter_dimension=0, tiled=True)

    sum_gate, sum_up, sum_down = (over_dp(g).astype(f32) for g in (grad_gate, grad_up, grad_down))
    part = over_dp(jnp.concatenate([grad_qkv, grad_out], axis=1))
    pair = jnp.stack([part[:, :query_width], part[:, qkv_width:]])
    pair = lax.psum_scatter(pair, "tensor", scatter_dimension=2, tiled=True).astype(f32)
    kv_part = lax.psum_scatter(
        part[:, query_width:qkv_width], "tensor", scatter_dimension=0, tiled=True
    ).astype(f32)
    small = lax.psum(jnp.concatenate([bias_term, gain_one_term, gain_two_term]), ("dp", "tensor"))
    place = lax.axis_index("dp") * tensor_size + rank
    devices = lax.axis_size("dp") * tensor_size

    def own(start, size):
        share = size // devices
        return lax.dynamic_slice_in_dim(small, start + place * share, share, 0)

    return (
        mixed,
        input_grad,
        own(qkv_width, model_width),
        pair[0],
        own(0, query_width),
        kv_part[:, :kv_width],
        small[query_width : query_width + kv_width],
        kv_part[:, kv_width:],
        small[query_width + kv_width : qkv_width],
        pair[1],
        own(qkv_width + model_width, model_width),
        sum_gate,
        sum_up,
        sum_down,
    )


def solution(mesh):
    both = ("dp", "tensor")
    return jax.shard_map(
        local,
        mesh=mesh,
        in_specs=(
            P(both, None),
            P("dp", None),
            P("dp"),
            P("dp", "tensor"),
            P("tensor"),
            P("dp", None),
            P(),
            P("dp", None),
            P(),
            P("dp", "tensor"),
            P("dp"),
            P("dp", "tensor"),
            P("dp", "tensor"),
            P("dp", "tensor"),
            P(both, None),
        ),
        out_specs=(
            P(both, None),
            P(both, None),
            P(both),
            P("dp", "tensor"),
            P(both),
            P(both, None),
            P(),
            P(both, None),
            P(),
            P("dp", "tensor"),
            P(both),
            P("dp", "tensor"),
            P("dp", "tensor"),
            P("dp", "tensor"),
        ),
        check_vma=False,
    )
```

profile of v0, /device:TPU:0, one launch (start us, length us, event | category | flops | bytes accessed | tf_op | source)
XLA Modules:
  0.0 1033.9 jit_solution(3349695426935198296)
XLA Ops:
  9.2 34.0 %all-gather.11.cloned.1.call-done = bf16[2,192,1536]{2,1,0:T(8,128)(2,1)} async-done(((bf16[2,192,384]{2,1,0:T(8,128)(2,1)}), bf16[2,192,1536]{2,1,0:T(8,128)(2,1)}) %all-gather.11.cloned.1.call-update) | async-done | bytes 1179664 | tf_op jit(solution)/shard_map/all_gather | solution.py:83
  46.7 8.9 all-gather
  55.7 11.9 %all-gather.1 = bf16[4,1,384]{2,1,0:T(2,128)(2,1)S(1)} all-gather(bf16[1,1,384]{2,1,0:T(2,128)(2,1)S(1)} %reshape.237), channel_id=1, replica_groups=mesh['dp'=8,'tensor'=4] {'tensor'}, dimensions={0}, use_global_device_ids=true | all-gather | bytes 3840 | tf_op jit(solution)/shard_map/all_gather | solution.py:90
  69.2 42.2 %all-gather.13.cloned.1.call-done = bf16[1536,3584]{1,0:T(8,128)(2,1)} async-done(((bf16[192,3584]{1,0:T(8,128)(2,1)}), bf16[1536,3584]{1,0:T(8,128)(2,1)}) %all-gather.13.cloned.1.call-update) | async-done | bytes 11010064 | tf_op jit(solution)/shard_map/all_gather | solution.py:85
  126.3 21.2 %all-gather.15.cloned.1.call-done = bf16[1024,512]{1,0:T(8,128)(2,1)} async-done(((bf16[256,512]{1,0:T(8,128)(2,1)}), bf16[1024,512]{1,0:T(8,128)(2,1)}) %all-gather.15.cloned.1.call-update) | async-done | bytes 1048592 | tf_op jit(solution)/shard_map/all_gather | solution.py:111
  168.2 29.2 %all-gather.19.cloned.1.call-done = bf16[1536,2240]{1,0:T(8,128)(2,1)} async-done(((bf16[192,2240]{1,0:T(8,128)(2,1)}), bf16[1536,2240]{1,0:T(8,128)(2,1)}) %all-gather.19.cloned.1.call-update) | async-done | bytes 6881296 | tf_op jit(solution)/shard_map/all_gather | solution.py:92
  197.4 65.5 %all-gather.17.cloned.1.call-done = bf16[1024,1536]{1,0:T(8,128)(2,1)} async-done(((bf16[256,1536]{1,0:T(8,128)(2,1)}), bf16[1024,1536]{1,0:T(8,128)(2,1)}) %all-gather.17.cloned.1.call-update) | async-done | bytes 3145744 | tf_op jit(solution)/shard_map/all_gather | solution.py:138
  262.8 13.2 %fusion.67 = f32[1024,2240]{0,1:T(8,128)} fusion(bf16[1024,1536]{1,0:T(8,128)(2,1)} %all-gather.17.cloned.1.call-done, bf16[1536,2240]{1,0:T(8,128)(2,1)} %all-gather.19.cloned.1.call-done), kind=kOutput, calls=%fused_computation.132 | convolution fusion | flops 7046430720 | bytes 19202048 | tf_op jit(solution)/shard_map/dot_general | solution.py:139
  276.0 35.9 %all-gather.21.cloned.1.call-done = bf16[1536,2240]{1,0:T(8,128)(2,1)} async-done(((bf16[192,2240]{1,0:T(8,128)(2,1)}), bf16[1536,2240]{1,0:T(8,128)(2,1)}) %all-gather.21.cloned.1.call-update) | async-done | bytes 6881296 | tf_op jit(solution)/shard_map/all_gather | solution.py:93
  312.0 13.3 %fusion.68 = f32[1024,2240]{0,1:T(8,128)} fusion(bf16[1024,1536]{1,0:T(8,128)(2,1)} %all-gather.17.cloned.1.call-done, bf16[1536,2240]{1,0:T(8,128)(2,1)} %all-gather.21.cloned.1.call-done), kind=kOutput, calls=%fused_computation.133 | convolution fusion | flops 7046430720 | bytes 19202048 | tf_op jit(solution)/shard_map/dot_general | solution.py:140
  325.3 51.8 %all-gather.25.cloned.1.call-done = bf16[1024,1536]{1,0:T(8,128)(2,1)} async-done(((bf16[256,1536]{1,0:T(8,128)(2,1)}), bf16[1024,1536]{1,0:T(8,128)(2,1)}) %all-gather.25.cloned.1.call-update) | async-done | bytes 3145744 | tf_op jit(solution)/shard_map/all_gather | solution.py:95
  377.0 49.3 %all-gather.23.cloned.1.call-done = bf16[1536,2240]{1,0:T(8,128)(2,1)} async-done(((bf16[192,2240]{1,0:T(8,128)(2,1)}), bf16[1536,2240]{1,0:T(8,128)(2,1)}) %all-gather.23.cloned.1.call-update) | async-done | bytes 6881296 | tf_op jit(solution)/shard_map/all_gather | solution.py:94
  426.3 20.5 %multiply_convert_fusion = (bf16[1024,2240]{0,1:T(8,128)(2,1)}, bf16[1024,2240]{0,1:T(8,128)(2,1)}, bf16[1024,2240]{0,1:T(8,128)(2,1)}) fusion(f32[1024,2240]{0,1:T(8,128)} %fusion.67, f32[1024,2240]{0,1:T(8,128)} %fusion.68, bf16[1024,1536]{1,0:T(8,128)(2,1)} %all-gather.25.cloned.1.call-done, bf16[1536,2240]{1,0:T(8,128)(2,1)} %all-gather.23.cloned.1.call-done), kind=kOutput, calls=%fused_computation.13 | convolution fusion | flops 7083130880 | bytes 42139648 | tf_op jit(solution)/shard_map/dot_general | solution.py:147
  446.8 11.4 %fusion.69 = f32[1024,1536]{1,0:T(8,128)S(1)} fusion(bf16[1024,2240]{0,1:T(8,128)(2,1)} %get-tuple-element.91, bf16[1536,2240]{1,0:T(8,128)(2,1)} %all-gather.19.cloned.1.call-done), kind=kOutput, calls=%fused_computation.134 | convolution fusion | flops 7046430720 | bytes 17760256 | tf_op jit(solution)/shard_map/dot_general | solution.py:37
  458.2 9.4 add_convert_fusion
  467.7 12.5 %convolution_convert_fusion.5 = bf16[1024,1536]{1,0:T(8,128)(2,1)} fusion(bf16[1024,2240]{0,1:T(8,128)(2,1)} %get-tuple-element.92, bf16[1536,2240]{1,0:T(8,128)(2,1)} %all-gather.23.cloned.1.call-done), kind=kOutput, calls=%fused_computation.30 | convolution fusion | flops 7048003584 | bytes 14614528 | tf_op jit(solution)/shard_map/dot_general | solution.py:37
  480.2 48.0 %reduce-scatter.16.cloned.1.call-done = bf16[256,1536]{1,0:T(8,128)(2,1)} async-done(((bf16[1024,1536]{1,0:T(8,128)(2,1)}), bf16[256,1536]{1,0:T(8,128)(2,1)}) %reduce-scatter.16.cloned.1.call-update) | async-done | bytes 786448 | tf_op jit(solution)/shard_map/reduce_scatter | solution.py:150
  530.5 60.1 %reduce-scatter.14.cloned.1.call-done = bf16[256,1536]{1,0:T(8,128)(2,1)} async-done(((bf16[1024,1536]{1,0:T(8,128)(2,1)}), bf16[256,1536]{1,0:T(8,128)(2,1)}) %reduce-scatter.14.cloned.1.call-update) | async-done | bytes 786448 | tf_op jit(solution)/shard_map/reduce_scatter | solution.py:143
  601.3 9.2 fusion.1
  616.7 11.1 %fusion.3 = bf16[2,6,256,768]{2,3,1,0:T(8,128)(2,1)} fusion(f32[2,768,256,6]{2,1,3,0:T(8,128)} %get-tuple-element.130, f32[2,768,256,6]{2,1,3,0:T(8,128)} %copy-done.2, f32[2,6,256]{2,1,0:T(8,128)S(1)} %get-tuple-element.129, f32[2,6,256]{2,1,0:T(8,128)S(1)} %copy-done.17, pred[256,768]{0,1:T(8,128)(4,1)S(1)} %compare_and_fusion), kind=kLoop, calls=%fused_computation.9 | loop fusion | flops 14155776 | bytes 23814144 | tf_op jit(solution)/shard_map/convert_element_type | solution.py:167
  634.6 7.8 dynamic_update_slice.3
  651.5 18.4 %reduce-scatter.18.cloned.1.call-done = bf16[256,512]{0,1:T(8,128)(2,1)} async-done(((bf16[1024,512]{0,1:T(8,128)(2,1)}), bf16[256,512]{0,1:T(8,128)(2,1)}) %reduce-scatter.18.cloned.1.call-update) | async-done | bytes 262160 | tf_op jit(solution)/shard_map/reduce_scatter | solution.py:184
  681.4 12.3 %fusion = bf16[1536,2240]{0,1:T(8,128)(2,1)} fusion(bf16[1024,2240]{0,1:T(8,128)(2,1)} %get-tuple-element.92, bf16[1024,1536]{1,0:T(8,128)(2,1)} %all-gather.25.cloned.1.call-done), kind=kOutput, calls=%fused_computation.4 | convolution fusion | flops 7049871360 | bytes 14614528 | tf_op jit(solution)/shard_map/dot_general | solution.py:37
  693.7 10.7 %copy.161 = bf16[1536,2240]{1,0:T(8,128)(2,1)} copy(bf16[1536,2240]{0,1:T(8,128)(2,1)} %fusion) | data formatting | bytes 13762560
  704.7 12.3 %convolution_convert_fusion.2 = bf16[1536,2240]{1,0:T(8,128)(2,1)} fusion(bf16[1024,1536]{1,0:T(8,128)(2,1)} %all-gather.17.cloned.1.call-done, bf16[1024,2240]{0,1:T(8,128)(2,1)} %get-tuple-element.91), kind=kOutput, calls=%fused_computation.2 | convolution fusion | flops 7049871360 | bytes 14614528 | tf_op jit(solution)/shard_map/dot_general | solution.py:37
  717.1 12.7 %convolution_convert_fusion.1 = bf16[1536,2240]{1,0:T(8,128)(2,1)} fusion(bf16[1024,1536]{1,0:T(8,128)(2,1)} %all-gather.17.cloned.1.call-done, bf16[1024,2240]{0,1:T(8,128)(2,1)} %get-tuple-element.90), kind=kOutput, calls=%fused_computation.1 | convolution fusion | flops 7049871360 | bytes 14614528 | tf_op jit(solution)/shard_map/dot_general | solution.py:37
  729.8 34.6 %reduce-scatter.20.cloned.1.call-done = bf16[192,3584]{1,0:T(8,128)(2,1)} async-done(((bf16[1536,3584]{1,0:T(8,128)(2,1)}), bf16[192,3584]{1,0:T(8,128)(2,1)}) %reduce-scatter.20.cloned.1.call-update) | async-done | bytes 1376272 | tf_op jit(solution)/shard_map/reduce_scatter | solution.py:201
  787.0 40.5 %psum.7 = f32[5120]{0:T(1024)S(1)} all-reduce(f32[5120]{0:T(1024)S(1)} %pad_maximum_fusion.13), channel_id=1, replica_groups=mesh['dp'=8,'tensor'=4] {'dp','tensor'}, use_global_device_ids=true, to_apply=%region_13.14 | all-reduce | flops 5120 | bytes 40960 | tf_op jit(solution)/shard_map/psum | solution.py:210
  837.8 65.5 %reduce-scatter.24.cloned.1.call-done = bf16[192,2240]{1,0:T(8,128)(2,1)} async-done(((bf16[1536,2240]{1,0:T(8,128)(2,1)}), bf16[192,2240]{1,0:T(8,128)(2,1)}) %reduce-scatter.24.cloned.1.call-update) | async-done | bytes 860176 | tf_op jit(solution)/shard_map/reduce_scatter | solution.py:201
  905.7 66.4 %reduce-scatter.26.cloned.1.call-done = bf16[192,2240]{1,0:T(8,128)(2,1)} async-done(((bf16[1536,2240]{1,0:T(8,128)(2,1)}), bf16[192,2240]{1,0:T(8,128)(2,1)}) %reduce-scatter.26.cloned.1.call-update) | async-done | bytes 860176 | tf_op jit(solution)/shard_map/reduce_scatter | solution.py:201
  974.6 19.8 %reduce-scatter.22.cloned.1.call-done = bf16[48,512]{1,0:T(8,128)(2,1)} async-done(((bf16[192,512]{1,0:T(8,128)(2,1)}), bf16[48,512]{1,0:T(8,128)(2,1)}) %reduce-scatter.22.cloned.1.call-update) | async-done | bytes 49168 | tf_op jit(solution)/shard_map/reduce_scatter | solution.py:207
  995.8 28.4 %reduce-scatter.28.cloned.1.call-done = bf16[384,384]{1,0:T(8,128)(2,1)} async-done(((bf16[1536,384]{1,0:T(8,128)(2,1)}), bf16[384,384]{1,0:T(8,128)(2,1)}) %reduce-scatter.28.cloned.1.call-update) | async-done | bytes 294928
  (192 shorter events, 131.1 us)
Async XLA Ops:
  7.2 113.1 %copy-start = (s32[1,1024]{1,0:T(1,128)S(1)}, s32[1,1024]{1,0:T(1,128)}, u32[]{:S(2)}) copy-start(s32[1,1024]{1,0:T(1,128)} %param.16) | copy-start | bytes 12292
  7.2 39.5 %copy-start.27 = (bf16[192]{0:T(256)(128)(2,1)S(1)}, bf16[192]{0:T(256)(128)(2,1)}, u32[]{:S(2)}) copy-start(bf16[192]{0:T(256)(128)(2,1)} %param.17) | copy-start | bytes 1156
  7.2 39.5 %copy-start.28 = (bf16[192]{0:T(256)(128)(2,1)S(1)}, bf16[192]{0:T(256)(128)(2,1)}, u32[]{:S(2)}) copy-start(bf16[192]{0:T(256)(128)(2,1)} %param.25) | copy-start | bytes 1156
  7.2 48.5 %copy-start.23 = (bf16[384]{0:T(512)(128)(2,1)S(1)}, bf16[384]{0:T(512)(128)(2,1)}, u32[]{:S(2)}) copy-start(bf16[384]{0:T(512)(128)(2,1)} %param.19) | copy-start | bytes 2308
  7.2 61.6 %copy-start.25 = (bf16[256]{0:T(256)(128)(2,1)S(1)}, bf16[256]{0:T(256)(128)(2,1)}, u32[]{:S(2)}) copy-start(bf16[256]{0:T(256)(128)(2,1)} %param.21) | copy-start | bytes 1540
  7.2 61.6 %copy-start.24 = (bf16[256]{0:T(256)(128)(2,1)S(1)}, bf16[256]{0:T(256)(128)(2,1)}, u32[]{:S(2)}) copy-start(bf16[256]{0:T(256)(128)(2,1)} %param.23) | copy-start | bytes 1540
  7.2 61.7 %copy-start.4 = (bf16[256,1536]{1,0:T(8,128)(2,1)S(1)}, bf16[256,1536]{1,0:T(8,128)(2,1)}, u32[]{:S(2)}) copy-start(bf16[256,1536]{1,0:T(8,128)(2,1)} %param.15) | copy-start | bytes 2359300
  7.3 35.9 %all-gather.11.cloned.1.call-start = ((), (), s32[]{:S(2)}) async-start(), calls=%async_computation.9 | async-start | bytes 1474560 | tf_op jit(solution)/shard_map/all_gather | solution.py:83
  9.1 102.3 %all-gather.13.cloned.1.call-start = ((), (), s32[]{:S(2)}) async-start(), calls=%async_computation.10 | async-start | bytes 12386304 | tf_op jit(solution)/shard_map/all_gather | solution.py:85
  46.6 100.9 %all-gather.15.cloned.1.call-start = ((), (), s32[]{:S(2)}) async-start(), calls=%async_computation.11 | async-start | bytes 1310720 | tf_op jit(solution)/shard_map/all_gather | solution.py:111
  68.7 49.0 %copy-start.11 = (f32[256,64]{1,0:T(8,128)}, f32[256,64]{1,0:T(8,128)S(1)}, u32[]{:S(2)}) copy-start(f32[256,64]{1,0:T(8,128)S(1)} %copy.116) | copy-start | bytes 196612
  68.9 47.2 %copy-start.18 = (f32[1536]{0:T(1024)}, f32[1536]{0:T(1024)S(1)}, u32[]{:S(2)}) copy-start(f32[1536]{0:T(1024)S(1)} %get-tuple-element.89) | copy-start | bytes 18436
  69.2 46.9 %copy-start.21 = (f32[256]{0:T(256)}, f32[256]{0:T(256)S(1)}, u32[]{:S(2)}) copy-start(f32[256]{0:T(256)S(1)} %add_rsqrt_fusion.1) | copy-start | bytes 3076
  119.4 78.0 %all-gather.19.cloned.1.call-start = ((), (), s32[]{:S(2)}) async-start(), calls=%async_computation.13 | async-start | bytes 7962624 | tf_op jit(solution)/shard_map/all_gather | solution.py:92
  120.0 142.9 %all-gather.17.cloned.1.call-start = ((), (), s32[]{:S(2)}) async-start(), calls=%async_computation.12 | async-start | bytes 3932160 | tf_op jit(solution)/shard_map/all_gather | solution.py:138
  125.9 27.7 %copy-start.5 = (bf16[256,12,64]{2,0,1:T(8,128)(2,1)}, bf16[256,12,64]{2,0,1:T(8,128)(2,1)S(1)}, u32[]{:S(2)}) copy-start(bf16[256,12,64]{2,0,1:T(8,128)(2,1)S(1)} %copy.119) | copy-start | bytes 1179652
  126.3 27.3 %copy-start.6 = (bf16[256,12,64]{2,0,1:T(8,128)(2,1)}, bf16[256,12,64]{2,0,1:T(8,128)(2,1)S(1)}, u32[]{:S(2)}) copy-start(bf16[256,12,64]{2,0,1:T(8,128)(2,1)S(1)} %copy.120) | copy-start | bytes 1179652
  164.3 363.9 %copy-start.3 = (f32[256,1536]{1,0:T(8,128)}, f32[256,1536]{1,0:T(8,128)S(1)}, u32[]{:S(2)}) copy-start(f32[256,1536]{1,0:T(8,128)S(1)} %get-tuple-element.128) | copy-start | bytes 4718596
  165.6 146.4 %all-gather.21.cloned.1.call-start = ((), (), s32[]{:S(2)}) async-start(), calls=%async_computation.14 | async-start | bytes 7962624 | tf_op jit(solution)/shard_map/all_gather | solution.py:93
  166.1 210.9 %all-gather.25.cloned.1.call-start = ((), (), s32[]{:S(2)}) async-start(), calls=%async_computation.17 | async-start | bytes 3932160 | tf_op jit(solution)/shard_map/all_gather | solution.py:95
  166.9 259.4 %all-gather.23.cloned.1.call-start = ((), (), s32[]{:S(2)}) async-start(), calls=%async_computation.15 | async-start | bytes 7962624 | tf_op jit(solution)/shard_map/all_gather | solution.py:94
  167.6 360.5 %reduce-scatter.16.cloned.1.call-start = ((), (), s32[]{:S(2)}) async-start(), calls=%async_computation.18 | async-start | bytes 3932160 | tf_op jit(solution)/shard_map/reduce_scatter | solution.py:150
  467.6 123.0 %reduce-scatter.14.cloned.1.call-start = ((), (), s32[]{:S(2)}) async-start(), calls=%async_computation.16 | async-start | bytes 3932160 | tf_op jit(solution)/shard_map/reduce_scatter | solution.py:143
  480.1 189.7 %reduce-scatter.18.cloned.1.call-start = ((), (), s32[]{:S(2)}) async-start(), calls=%async_computation.19 | async-start | bytes 1310720 | tf_op jit(solution)/shard_map/reduce_scatter | solution.py:184
  642.5 122.0 %reduce-scatter.20.cloned.1.call-start = ((), (), s32[]{:S(2)}) async-start(), calls=%async_computation.20 | async-start | bytes 12386304 | tf_op jit(solution)/shard_map/reduce_scatter | solution.py:201
  647.9 25.0 %copy-start.22 = (f32[256]{0:T(256)S(1)}, f32[256]{0:T(256)}, u32[]{:S(2)}) copy-start(f32[256]{0:T(256)} %copy-done.21) | copy-start | bytes 3076
  681.4 153.0 %reduce-scatter.30.cloned.1.call-start = ((), (), s32[]{:S(2)}) async-start(), calls=%async_computation.25 | async-start | bytes 7962624
  704.4 198.8 %reduce-scatter.24.cloned.1.call-start = ((), (), s32[]{:S(2)}) async-start(), calls=%async_computation.22 | async-start | bytes 7962624 | tf_op jit(solution)/shard_map/reduce_scatter | solution.py:201
  717.0 255.1 %reduce-scatter.26.cloned.1.call-start = ((), (), s32[]{:S(2)}) async-start(), calls=%async_computation.23 | async-start | bytes 7962624 | tf_op jit(solution)/shard_map/reduce_scatter | solution.py:201
  729.8 264.6 %reduce-scatter.22.cloned.1.call-start = ((), (), s32[]{:S(2)}) async-start(), calls=%async_computation.21 | async-start | bytes 245760 | tf_op jit(solution)/shard_map/reduce_scatter | solution.py:207
  766.1 258.1 %reduce-scatter.28.cloned.1.call-start = ((), (), s32[]{:S(2)}) async-start(), calls=%async_computation.24 | async-start | bytes 1474560
  836.1 191.0 %copy-start.1 = (s32[1,1024]{1,0:T(1,128)S(1)}, s32[1,1024]{1,0:T(1,128)}, u32[]{:S(2)}) copy-start(s32[1,1024]{1,0:T(1,128)} %param.16) | copy-start | bytes 12292
  (17 other events, 145.8 us)
Sparse Core Ops, SparseCore 0:
  10.2 32.8 all-gather.10
  46.7 64.6 all-gather.12
  119.5 27.9 all-gather.14
  149.3 48.0 all-gather.18
  199.4 63.4 all-gather.16
  264.6 47.3 all-gather.20
  313.5 63.4 all-gather.24
  378.9 47.3 all-gather.22
  467.7 60.3 reduce-scatter.15
  530.3 60.3 reduce-scatter.13
  642.6 27.1 reduce-scatter.17
  681.5 82.8 reduce-scatter.19
  767.9 66.3 reduce-scatter.29
  837.7 65.4 reduce-scatter.23
  906.6 65.4 reduce-scatter.25
  974.8 19.5 reduce-scatter.21
  996.6 27.5 reduce-scatter.27
where the time goes:
time: 1040 us; the launch traced here: 1030 us
  waiting for transfers between devices  676 us (65%)
  matrix products  173 us (17%)
  blocking collectives  61.3 us (6%)
  local copies, waits for them, and re-layouts  59.8 us (6%)
  other arithmetic  46.9 us (5%)
  between operations  15 us (1%)
    reduce_scatter x3, waiting for transfers between devices, over_dp(): return lax.psum_scatter(grad, 'dp', scatter_dimension=0, tiled=True)  166 us
    dot_general x10, matrix products, dot_f32(): lax.dot_general(left, right, (dims, ((), ())), preferred_element_type=jnp...  88.6 us
    all_gather x1, waiting for transfers between devices, local(): rows_two = lax.all_gather(normed_two, 'tensor', axis=0, tiled=True)  65.5 us
    reduce_scatter x1, waiting for transfers between devices, local(): lax.psum_scatter(contract_cols(hidden_low, full_down).astype(bf16), 'tens...  60.1 us
    all_gather x1, waiting for transfers between devices, local(): cot_rows = lax.all_gather(cotangent, 'tensor', axis=0, tiled=True)  51.8 us
    all_gather x1, waiting for transfers between devices, local(): full_down = lax.all_gather(down_w, 'dp', axis=0, tiled=True)  49.3 us
    reduce_scatter x1, waiting for transfers between devices, local(): lax.psum_scatter((contract_cols(d_gate, full_gate) + contract_cols(d_uppe...  48 us
    all_gather x1, waiting for transfers between devices, local(): joined = lax.all_gather(joined, 'dp', axis=0, tiled=True)  42.2 us
  transfers between devices with their start and end apart: 17, of which 17 were waited for; matrix products, arithmetic and copies ran while one was open for 15% of the time, Pallas kernels for 0%

commit v1 on v0

--- a/solution.py
+++ b/solution.py
@@ -1,3 +1,4 @@
+import functools
 import jax
 import jax.numpy as jnp
 from jax import lax
@@ -9,6 +10,26 @@
 EPSILON = 1e-06
 ROPE_BASE = 1000000.0
 NEGATIVE = -1e30
+
+
+def carry_waves(mine_x, axis_key, dim_no):
+    n_parts = lax.axis_size(axis_key)
+    crops = [(kk, (kk + 1) % n_parts) for kk in range(n_parts)]
+    sides = [(kk, (kk - 1) % n_parts) for kk in range(n_parts)]
+    found_now, z_new = ([mine_x], [mine_x])
+    for _ in range(n_parts // 2):
+        y2 = lax.ppermute(found_now[-1], axis_key, crops)
+        found_now.append(y2)
+    for _ in range((n_parts - 1) // 2):
+        left_arr = lax.ppermute(z_new[-1], axis_key, sides)
+        z_new.append(left_arr)
+    earlier = jnp.concatenate([*found_now[::-1], *z_new[1:]], axis=dim_no)
+    return jnp.roll(
+        earlier, (lax.axis_index(axis_key) - n_parts // 2) * mine_x.shape[dim_no], axis=dim_no
+    )
+
+
+draft_the_ladders = functools.partial(carry_waves, axis_key="tensor", dim_no=0)
 
 
 def angle_tables(first, length, head_width):
@@ -92,7 +113,7 @@
     full_gate = lax.all_gather(gate_w, "dp", axis=0, tiled=True)
     full_up = lax.all_gather(up_w, "dp", axis=0, tiled=True)
     full_down = lax.all_gather(down_w, "dp", axis=0, tiled=True)
-    cot_rows = lax.all_gather(cotangent, "tensor", axis=0, tiled=True)
+    cot_rows = draft_the_ladders(cotangent)
     inputs = tokens.astype(f32)
     inverse_one = lax.rsqrt(jnp.mean(inputs * inputs, axis=-1, keepdims=True) + EPSILON)
     unit_one = inputs * inverse_one

time: 1040 us -> 988 us (0.950)
  waiting for transfers between devices: 676 us -> 614 us
    ppermute x0 -> x3, waiting for transfers between devices: none -> 72.9 us  [the longest x2 37.6 us: carry_waves(): y2 = lax.ppermute(found_now[-1], axis_key, crops)]
    all_gather x1, waiting for transfers between devices: 65.5 us -> 12.8 us  [local(): rows_two = lax.all_gather(normed_two, 'tensor', axis=0, tiled=True)]
    all_gather x1 -> x0, waiting for transfers between devices: 51.8 us -> none  [local(): cot_rows = lax.all_gather(cotangent, 'tensor', axis=0, tiled=True)]
    all_gather x1, waiting for transfers between devices: 29.2 us -> 0.01 us  [local(): full_gate = lax.all_gather(gate_w, 'dp', axis=0, tiled=True)]
    reduce_scatter x3 -> x4, waiting for transfers between devices: 166 us -> 180 us  [over_dp(): return lax.psum_scatter(grad, 'dp', scatter_dimension=0, tiled=True)]
    all_gather x1, waiting for transfers between devices: 49.3 us -> 37.4 us  [local(): full_down = lax.all_gather(down_w, 'dp', axis=0, tiled=True)]
    unnamed x19 -> x17, waiting for transfers between devices: 33.9 us -> 30.3 us
    unnamed x76 -> x82, local copies, waits for them, and re-layouts: 29.4 us -> 28.7 us
  transfers between devices with their start and end apart: 17 -> 19, of which waited for: 17 -> 18; matrix products, arithmetic and copies ran while one was open for 15% -> 17% of each run, Pallas kernels for 0% -> 0%
where the time goes in v1:
time: 988 us; the launch traced here: 983 us
  waiting for transfers between devices  614 us (62%)
  matrix products  175 us (18%)
  blocking collectives  61.4 us (6%)
  local copies, waits for them, and re-layouts  61.2 us (6%)
  other arithmetic  49.4 us (5%)
  between operations  15 us (2%)
    reduce_scatter x4, waiting for transfers between devices, over_dp(): return lax.psum_scatter(grad, 'dp', scatter_dimension=0, tiled=True)  180 us
    dot_general x10, matrix products, dot_f32(): lax.dot_general(left, right, (dims, ((), ())), preferred_element_type=jnp...  89.8 us
    reduce_scatter x1, waiting for transfers between devices, local(): lax.psum_scatter(contract_cols(hidden_low, full_down).astype(bf16), 'tens...  60.3 us
    reduce_scatter x1, waiting for transfers between devices, local(): lax.psum_scatter((contract_cols(d_gate, full_gate) + contract_cols(d_uppe...  47.9 us
    all_gather x1, waiting for transfers between devices, local(): joined = lax.all_gather(joined, 'dp', axis=0, tiled=True)  42.2 us
    psum x1, blocking collectives, local(): lax.psum(jnp.concatenate([bias_term, gain_one_term, gain_two_term]), ('dp...  40.6 us
    ppermute x2, waiting for transfers between devices, carry_waves(): y2 = lax.ppermute(found_now[-1], axis_key, crops)  37.6 us
    all_gather x1, waiting for transfers between devices, local(): full_down = lax.all_gather(down_w, 'dp', axis=0, tiled=True)  37.4 us
  transfers between devices with their start and end apart: 19, of which 18 were waited for; matrix products, arithmetic and copies ran while one was open for 17% of the time, Pallas kernels for 0%

profile of v1, /device:TPU:0, one launch (start us, length us, event | category | flops | bytes accessed | tf_op | source)
XLA Modules:
  0.0 982.8 jit_solution(1486486138218312664)
XLA Ops:
  9.2 34.0 %all-gather.10.cloned.1.call-done = bf16[2,192,1536]{2,1,0:T(8,128)(2,1)} async-done(((bf16[2,192,384]{2,1,0:T(8,128)(2,1)}), bf16[2,192,1536]{2,1,0:T(8,128)(2,1)}) %all-gather.10.cloned.1.call-update) | async-done | bytes 1179664 | tf_op jit(solution)/shard_map/all_gather | solution.py:104
  46.7 8.9 all-gather
  55.7 11.9 %all-gather.1 = bf16[4,1,384]{2,1,0:T(2,128)(2,1)S(1)} all-gather(bf16[1,1,384]{2,1,0:T(2,128)(2,1)S(1)} %reshape.237), channel_id=1, replica_groups=mesh['dp'=8,'tensor'=4] {'tensor'}, dimensions={0}, use_global_device_ids=true | all-gather | bytes 3840 | tf_op jit(solution)/shard_map/all_gather | solution.py:111
  69.2 42.2 %all-gather.12.cloned.1.call-done = bf16[1536,3584]{1,0:T(8,128)(2,1)} async-done(((bf16[192,3584]{1,0:T(8,128)(2,1)}), bf16[1536,3584]{1,0:T(8,128)(2,1)}) %all-gather.12.cloned.1.call-update) | async-done | bytes 11010064 | tf_op jit(solution)/shard_map/all_gather | solution.py:106
  126.3 21.2 %all-gather.14.cloned.1.call-done = bf16[1024,512]{1,0:T(8,128)(2,1)} async-done(((bf16[256,512]{1,0:T(8,128)(2,1)}), bf16[1024,512]{1,0:T(8,128)(2,1)}) %all-gather.14.cloned.1.call-update) | async-done | bytes 1048592 | tf_op jit(solution)/shard_map/all_gather | solution.py:132
  168.3 19.4 %collective-permute-done = bf16[256,1536]{1,0:T(8,128)(2,1)} collective-permute-done((bf16[256,1536]{1,0:T(8,128)(2,1)}, bf16[256,1536]{1,0:T(8,128)(2,1)}, u32[]{:S(2)}, u32[]{:S(2)}) %collective-permute-start) | collective-permute-done | bytes 786464 | tf_op jit(solution)/shard_map/ppermute | solution.py:21
  192.0 18.2 %collective-permute-done.1 = bf16[256,1536]{1,0:T(8,128)(2,1)} collective-permute-done((bf16[256,1536]{1,0:T(8,128)(2,1)}, bf16[256,1536]{1,0:T(8,128)(2,1)}, u32[]{:S(2)}, u32[]{:S(2)}) %collective-permute-start.1) | collective-permute-done | bytes 786464 | tf_op jit(solution)/shard_map/ppermute | solution.py:21
  216.4 35.3 %collective-permute-done.2 = bf16[256,1536]{1,0:T(8,128)(2,1)} collective-permute-done((bf16[256,1536]{1,0:T(8,128)(2,1)}, bf16[256,1536]{1,0:T(8,128)(2,1)}, u32[]{:S(2)}, u32[]{:S(2)}) %collective-permute-start.2) | collective-permute-done | bytes 786464 | tf_op jit(solution)/shard_map/ppermute | solution.py:24
  261.0 12.8 %all-gather.16.cloned.1.call-done = bf16[1024,1536]{1,0:T(8,128)(2,1)} async-done(((bf16[256,1536]{1,0:T(8,128)(2,1)}), bf16[1024,1536]{1,0:T(8,128)(2,1)}) %all-gather.16.cloned.1.call-update) | async-done | bytes 3145744 | tf_op jit(solution)/shard_map/all_gather | solution.py:159
  273.8 13.2 %fusion.71 = f32[1024,2240]{0,1:T(8,128)} fusion(bf16[1024,1536]{1,0:T(8,128)(2,1)} %all-gather.16.cloned.1.call-done, bf16[1536,2240]{1,0:T(8,128)(2,1)} %all-gather.18.cloned.1.call-done), kind=kOutput, calls=%fused_computation.144 | convolution fusion | flops 7046430720 | bytes 19202048 | tf_op jit(solution)/shard_map/dot_general | solution.py:160
  287.0 37.2 %all-gather.20.cloned.1.call-done = bf16[1536,2240]{1,0:T(8,128)(2,1)} async-done(((bf16[192,2240]{1,0:T(8,128)(2,1)}), bf16[1536,2240]{1,0:T(8,128)(2,1)}) %all-gather.20.cloned.1.call-update) | async-done | bytes 6881296 | tf_op jit(solution)/shard_map/all_gather | solution.py:114
  324.2 13.2 %fusion.72 = f32[1024,2240]{0,1:T(8,128)} fusion(bf16[1024,1536]{1,0:T(8,128)(2,1)} %all-gather.16.cloned.1.call-done, bf16[1536,2240]{1,0:T(8,128)(2,1)} %all-gather.20.cloned.1.call-done), kind=kOutput, calls=%fused_computation.145 | convolution fusion | flops 7046430720 | bytes 19202048 | tf_op jit(solution)/shard_map/dot_general | solution.py:161
  337.4 37.4 %all-gather.22.cloned.1.call-done = bf16[1536,2240]{1,0:T(8,128)(2,1)} async-done(((bf16[192,2240]{1,0:T(8,128)(2,1)}), bf16[1536,2240]{1,0:T(8,128)(2,1)}) %all-gather.22.cloned.1.call-update) | async-done | bytes 6881296 | tf_op jit(solution)/shard_map/all_gather | solution.py:115
  374.8 20.9 %multiply_convert_fusion = (bf16[1024,2240]{0,1:T(8,128)(2,1)}, bf16[1024,2240]{0,1:T(8,128)(2,1)}, bf16[1024,2240]{0,1:T(8,128)(2,1)}) fusion(f32[1024,2240]{0,1:T(8,128)} %fusion.71, f32[1024,2240]{0,1:T(8,128)} %fusion.72, bf16[1536,2240]{1,0:T(8,128)(2,1)} %all-gather.22.cloned.1.call-done, bf16[2048,1536]{1,0:T(8,128)(2,1)} %constant_dynamic-update-slice_fusion, ...), kind=kOutput, calls=%fused_computation.12 | convolution fusion | flops 7083130880 | bytes 42336260 | tf_op jit(solution)/shard_map/dot_general | solution.py:168
  395.8 11.4 %fusion.73 = f32[1024,1536]{1,0:T(8,128)S(1)} fusion(bf16[1024,2240]{0,1:T(8,128)(2,1)} %get-tuple-element.21, bf16[1536,2240]{1,0:T(8,128)(2,1)} %all-gather.18.cloned.1.call-done), kind=kOutput, calls=%fused_computation.146 | convolution fusion | flops 7046430720 | bytes 17760256 | tf_op jit(solution)/shard_map/dot_general | solution.py:58
  407.2 9.3 add_convert_fusion
  416.5 12.4 %convolution_convert_fusion.5 = bf16[1024,1536]{1,0:T(8,128)(2,1)} fusion(bf16[1024,2240]{0,1:T(8,128)(2,1)} %get-tuple-element.22, bf16[1536,2240]{1,0:T(8,128)(2,1)} %all-gather.22.cloned.1.call-done), kind=kOutput, calls=%fused_computation.29 | convolution fusion | flops 7048003584 | bytes 14614528 | tf_op jit(solution)/shard_map/dot_general | solution.py:58
  429.0 47.9 %reduce-scatter.14.cloned.1.call-done = bf16[256,1536]{1,0:T(8,128)(2,1)} async-done(((bf16[1024,1536]{1,0:T(8,128)(2,1)}), bf16[256,1536]{1,0:T(8,128)(2,1)}) %reduce-scatter.14.cloned.1.call-update) | async-done | bytes 786448 | tf_op jit(solution)/shard_map/reduce_scatter | solution.py:171
  479.3 60.3 %reduce-scatter.12.cloned.1.call-done = bf16[256,1536]{1,0:T(8,128)(2,1)} async-done(((bf16[1024,1536]{1,0:T(8,128)(2,1)}), bf16[256,1536]{1,0:T(8,128)(2,1)}) %reduce-scatter.12.cloned.1.call-update) | async-done | bytes 786448 | tf_op jit(solution)/shard_map/reduce_scatter | solution.py:164
  550.1 9.2 fusion
  565.6 11.2 %fusion.2 = bf16[2,6,256,768]{2,3,1,0:T(8,128)(2,1)} fusion(f32[2,768,256,6]{2,1,3,0:T(8,128)} %get-tuple-element.60, f32[2,768,256,6]{2,1,3,0:T(8,128)} %copy-done.2, f32[2,6,256]{2,1,0:T(8,128)S(1)} %get-tuple-element.59, f32[2,6,256]{2,1,0:T(8,128)S(1)} %copy-done.18, pred[256,768]{0,1:T(8,128)(4,1)S(1)} %compare_and_fusion), kind=kLoop, calls=%fused_computation.8 | loop fusion | flops 14155776 | bytes 23814144 | tf_op jit(solution)/shard_map/convert_element_type | solution.py:188
  583.5 7.8 dynamic_update_slice.3
  600.3 18.3 %reduce-scatter.16.cloned.1.call-done = bf16[256,512]{0,1:T(8,128)(2,1)} async-done(((bf16[1024,512]{0,1:T(8,128)(2,1)}), bf16[256,512]{0,1:T(8,128)(2,1)}) %reduce-scatter.16.cloned.1.call-update) | async-done | bytes 262160 | tf_op jit(solution)/shard_map/reduce_scatter | solution.py:205
  630.2 12.7 %convolution_convert_fusion = bf16[1536,2240]{1,0:T(8,128)(2,1)} fusion(bf16[1024,2240]{0,1:T(8,128)(2,1)} %get-tuple-element.22, bf16[2048,1536]{1,0:T(8,128)(2,1)} %constant_dynamic-update-slice_fusion, s32[]{:T(128)S(6)} %select_n.35), kind=kOutput, calls=%fused_computation | convolution fusion | flops 7049871360 | bytes 14614532 | tf_op jit(solution)/shard_map/dot_general | solution.py:58
  643.2 13.6 %convolution_convert_fusion.2 = bf16[1536,2240]{1,0:T(8,128)(2,1)} fusion(bf16[1024,1536]{1,0:T(8,128)(2,1)} %all-gather.16.cloned.1.call-done, bf16[1024,2240]{0,1:T(8,128)(2,1)} %get-tuple-element.21), kind=kOutput, calls=%fused_computation.2 | convolution fusion | flops 7049871360 | bytes 14614528 | tf_op jit(solution)/shard_map/dot_general | solution.py:58
  656.9 12.4 %convolution_convert_fusion.1 = bf16[1536,2240]{1,0:T(8,128)(2,1)} fusion(bf16[1024,1536]{1,0:T(8,128)(2,1)} %all-gather.16.cloned.1.call-done, bf16[1024,2240]{0,1:T(8,128)(2,1)} %get-tuple-element.20), kind=kOutput, calls=%fused_computation.1 | convolution fusion | flops 7049871360 | bytes 14614528 | tf_op jit(solution)/shard_map/dot_general | solution.py:58
  669.4 43.9 %reduce-scatter.18.cloned.1.call-done = bf16[192,3584]{1,0:T(8,128)(2,1)} async-done(((bf16[1536,3584]{1,0:T(8,128)(2,1)}), bf16[192,3584]{1,0:T(8,128)(2,1)}) %reduce-scatter.18.cloned.1.call-update) | async-done | bytes 1376272 | tf_op jit(solution)/shard_map/reduce_scatter | solution.py:222
  735.8 40.6 %psum.7 = f32[5120]{0:T(1024)S(1)} all-reduce(f32[5120]{0:T(1024)S(1)} %pad_maximum_fusion.13), channel_id=1, replica_groups=mesh['dp'=8,'tensor'=4] {'dp','tensor'}, use_global_device_ids=true, to_apply=%region_13.14 | all-reduce | flops 5120 | bytes 40960 | tf_op jit(solution)/shard_map/psum | solution.py:231
  785.5 66.5 %reduce-scatter.22.cloned.1.call-done = bf16[192,2240]{1,0:T(8,128)(2,1)} async-done(((bf16[1536,2240]{1,0:T(8,128)(2,1)}), bf16[192,2240]{1,0:T(8,128)(2,1)}) %reduce-scatter.22.cloned.1.call-update) | async-done | bytes 860176 | tf_op jit(solution)/shard_map/reduce_scatter | solution.py:222
  854.6 66.4 %reduce-scatter.24.cloned.1.call-done = bf16[192,2240]{1,0:T(8,128)(2,1)} async-done(((bf16[1536,2240]{1,0:T(8,128)(2,1)}), bf16[192,2240]{1,0:T(8,128)(2,1)}) %reduce-scatter.24.cloned.1.call-update) | async-done | bytes 860176 | tf_op jit(solution)/shard_map/reduce_scatter | solution.py:222
  923.5 19.8 %reduce-scatter.20.cloned.1.call-done = bf16[48,512]{1,0:T(8,128)(2,1)} async-done(((bf16[192,512]{1,0:T(8,128)(2,1)}), bf16[48,512]{1,0:T(8,128)(2,1)}) %reduce-scatter.20.cloned.1.call-update) | async-done | bytes 49168 | tf_op jit(solution)/shard_map/reduce_scatter | solution.py:228
  944.7 28.4 %reduce-scatter.28.cloned.1.call-done = bf16[384,384]{1,0:T(8,128)(2,1)} async-done(((bf16[1536,384]{1,0:T(8,128)(2,1)}), bf16[384,384]{1,0:T(8,128)(2,1)}) %reduce-scatter.28.cloned.1.call-update) | async-done | bytes 294928
  (203 shorter events, 149.7 us)
Async XLA Ops:
  7.2 113.1 %copy-start = (s32[1,1024]{1,0:T(1,128)S(1)}, s32[1,1024]{1,0:T(1,128)}, u32[]{:S(2)}) copy-start(s32[1,1024]{1,0:T(1,128)} %param.16) | copy-start | bytes 12292
  7.2 39.5 %copy-start.28 = (bf16[192]{0:T(256)(128)(2,1)S(1)}, bf16[192]{0:T(256)(128)(2,1)}, u32[]{:S(2)}) copy-start(bf16[192]{0:T(256)(128)(2,1)} %param.17) | copy-start | bytes 1156
  7.2 39.5 %copy-start.29 = (bf16[192]{0:T(256)(128)(2,1)S(1)}, bf16[192]{0:T(256)(128)(2,1)}, u32[]{:S(2)}) copy-start(bf16[192]{0:T(256)(128)(2,1)} %param.25) | copy-start | bytes 1156
  7.2 48.5 %copy-start.24 = (bf16[384]{0:T(512)(128)(2,1)S(1)}, bf16[384]{0:T(512)(128)(2,1)}, u32[]{:S(2)}) copy-start(bf16[384]{0:T(512)(128)(2,1)} %param.19) | copy-start | bytes 2308
  7.2 61.6 %copy-start.26 = (bf16[256]{0:T(256)(128)(2,1)S(1)}, bf16[256]{0:T(256)(128)(2,1)}, u32[]{:S(2)}) copy-start(bf16[256]{0:T(256)(128)(2,1)} %param.21) | copy-start | bytes 1540
  7.2 61.6 %copy-start.25 = (bf16[256]{0:T(256)(128)(2,1)S(1)}, bf16[256]{0:T(256)(128)(2,1)}, u32[]{:S(2)}) copy-start(bf16[256]{0:T(256)(128)(2,1)} %param.23) | copy-start | bytes 1540
  7.2 61.7 %copy-start.4 = (bf16[256,1536]{1,0:T(8,128)(2,1)S(1)}, bf16[256,1536]{1,0:T(8,128)(2,1)}, u32[]{:S(2)}) copy-start(bf16[256,1536]{1,0:T(8,128)(2,1)} %param.15) | copy-start | bytes 2359300
  7.3 35.9 %all-gather.10.cloned.1.call-start = ((), (), s32[]{:S(2)}) async-start(), calls=%async_computation.9 | async-start | bytes 1474560 | tf_op jit(solution)/shard_map/all_gather | solution.py:104
  9.1 102.3 %all-gather.12.cloned.1.call-start = ((), (), s32[]{:S(2)}) async-start(), calls=%async_computation.10 | async-start | bytes 12386304 | tf_op jit(solution)/shard_map/all_gather | solution.py:106
  46.6 100.9 %all-gather.14.cloned.1.call-start = ((), (), s32[]{:S(2)}) async-start(), calls=%async_computation.11 | async-start | bytes 1310720 | tf_op jit(solution)/shard_map/all_gather | solution.py:132
  68.8 49.0 %copy-start.12 = (f32[256,64]{1,0:T(8,128)}, f32[256,64]{1,0:T(8,128)S(1)}, u32[]{:S(2)}) copy-start(f32[256,64]{1,0:T(8,128)S(1)} %copy.112) | copy-start | bytes 196612
  68.9 47.2 %copy-start.19 = (f32[1536]{0:T(1024)}, f32[1536]{0:T(1024)S(1)}, u32[]{:S(2)}) copy-start(f32[1536]{0:T(1024)S(1)} %get-tuple-element.19) | copy-start | bytes 18436
  69.2 46.9 %copy-start.22 = (f32[256]{0:T(256)}, f32[256]{0:T(256)S(1)}, u32[]{:S(2)}) copy-start(f32[256]{0:T(256)S(1)} %add_rsqrt_fusion.1) | copy-start | bytes 3076
  119.4 141.6 %all-gather.18.cloned.1.call-start = ((), (), s32[]{:S(2)}) async-start(), calls=%async_computation.13 | async-start | bytes 7962624 | tf_op jit(solution)/shard_map/all_gather | solution.py:113
  120.0 153.8 %all-gather.16.cloned.1.call-start = ((), (), s32[]{:S(2)}) async-start(), calls=%async_computation.12 | async-start | bytes 3932160 | tf_op jit(solution)/shard_map/all_gather | solution.py:159
  164.3 312.7 %copy-start.3 = (f32[256,1536]{1,0:T(8,128)}, f32[256,1536]{1,0:T(8,128)S(1)}, u32[]{:S(2)}) copy-start(f32[256,1536]{1,0:T(8,128)S(1)} %get-tuple-element.58) | copy-start | bytes 4718596
  165.6 158.6 %all-gather.20.cloned.1.call-start = ((), (), s32[]{:S(2)}) async-start(), calls=%async_computation.14 | async-start | bytes 7962624 | tf_op jit(solution)/shard_map/all_gather | solution.py:114
  166.2 208.6 %all-gather.22.cloned.1.call-start = ((), (), s32[]{:S(2)}) async-start(), calls=%async_computation.15 | async-start | bytes 7962624 | tf_op jit(solution)/shard_map/all_gather | solution.py:115
  166.9 310.0 %reduce-scatter.14.cloned.1.call-start = ((), (), s32[]{:S(2)}) async-start(), calls=%async_computation.17 | async-start | bytes 3932160 | tf_op jit(solution)/shard_map/reduce_scatter | solution.py:171
  167.0 20.7 %collective-permute-start = (bf16[256,1536]{1,0:T(8,128)(2,1)}, bf16[256,1536]{1,0:T(8,128)(2,1)}, u32[]{:S(2)}, u32[]{:S(2)}) collective-permute-start(bf16[256,1536]{1,0:T(8,128)(2,1)} %param.29), channel_id=1, source_target_pairs={{0,1},{1,2},{2,3},{3,0},{4,5},{5,6},{6,7},{7,4},{8,9},{9,10},{10,1... | collective-permute-start | bytes 2359304 | tf_op jit(solution)/shard_map/ppermute | solution.py:21
  187.6 22.5 %collective-permute-start.1 = (bf16[256,1536]{1,0:T(8,128)(2,1)}, bf16[256,1536]{1,0:T(8,128)(2,1)}, u32[]{:S(2)}, u32[]{:S(2)}) collective-permute-start(bf16[256,1536]{1,0:T(8,128)(2,1)} %collective-permute-done), channel_id=1, source_target_pairs={{0,1},{1,2},{2,3},{3,0},{4,5},{5,6},{6,7},{7,4},{8,9},{9,10},{10,1... | collective-permute-start | bytes 2359304 | tf_op jit(solution)/shard_map/ppermute | solution.py:21
  187.6 64.0 %collective-permute-start.2 = (bf16[256,1536]{1,0:T(8,128)(2,1)}, bf16[256,1536]{1,0:T(8,128)(2,1)}, u32[]{:S(2)}, u32[]{:S(2)}) collective-permute-start(bf16[256,1536]{1,0:T(8,128)(2,1)} %param.29), channel_id=1, source_target_pairs={{0,3},{1,0},{2,1},{3,2},{4,7},{5,4},{6,5},{7,6},{8,11},{9,8},{10,9... | collective-permute-start | bytes 2359304 | tf_op jit(solution)/shard_map/ppermute | solution.py:24
  192.0 65.9 %copy-start.7 = (bf16[256,1536]{1,0:T(8,128)(2,1)S(1)}, bf16[256,1536]{1,0:T(8,128)(2,1)}, u32[]{:S(2)}) copy-start(bf16[256,1536]{1,0:T(8,128)(2,1)} %param.29) | copy-start | bytes 2359300
  416.5 123.1 %reduce-scatter.12.cloned.1.call-start = ((), (), s32[]{:S(2)}) async-start(), calls=%async_computation.16 | async-start | bytes 3932160 | tf_op jit(solution)/shard_map/reduce_scatter | solution.py:164
  429.0 189.7 %reduce-scatter.16.cloned.1.call-start = ((), (), s32[]{:S(2)}) async-start(), calls=%async_computation.18 | async-start | bytes 1310720 | tf_op jit(solution)/shard_map/reduce_scatter | solution.py:205
  591.3 121.9 %reduce-scatter.18.cloned.1.call-start = ((), (), s32[]{:S(2)}) async-start(), calls=%async_computation.19 | async-start | bytes 12386304 | tf_op jit(solution)/shard_map/reduce_scatter | solution.py:222
  630.2 152.8 %reduce-scatter.26.cloned.1.call-start = ((), (), s32[]{:S(2)}) async-start(), calls=%async_computation.23 | async-start | bytes 7962624 | tf_op jit(solution)/shard_map/reduce_scatter | solution.py:222
  643.0 209.1 %reduce-scatter.22.cloned.1.call-start = ((), (), s32[]{:S(2)}) async-start(), calls=%async_computation.21 | async-start | bytes 7962624 | tf_op jit(solution)/shard_map/reduce_scatter | solution.py:222
  656.9 264.1 %reduce-scatter.24.cloned.1.call-start = ((), (), s32[]{:S(2)}) async-start(), calls=%async_computation.22 | async-start | bytes 7962624 | tf_op jit(solution)/shard_map/reduce_scatter | solution.py:222
  669.3 274.0 %reduce-scatter.20.cloned.1.call-start = ((), (), s32[]{:S(2)}) async-start(), calls=%async_computation.20 | async-start | bytes 245760 | tf_op jit(solution)/shard_map/reduce_scatter | solution.py:228
  714.9 258.2 %reduce-scatter.28.cloned.1.call-start = ((), (), s32[]{:S(2)}) async-start(), calls=%async_computation.24 | async-start | bytes 1474560
  783.0 192.9 %copy-start.1 = (s32[1,1024]{1,0:T(1,128)S(1)}, s32[1,1024]{1,0:T(1,128)}, u32[]{:S(2)}) copy-start(s32[1,1024]{1,0:T(1,128)} %param.16) | copy-start | bytes 12292
  (20 other events, 225.7 us)
Sparse Core Ops, SparseCore 0:
  10.2 32.8 all-gather.9
  46.7 64.6 all-gather.11
  119.5 27.9 all-gather.13
  149.2 48.0 all-gather.17
  199.4 74.3 all-gather.15
  275.5 48.6 all-gather.19
  326.1 48.7 all-gather.21
  416.6 60.2 reduce-scatter.13
  479.2 60.3 reduce-scatter.11
  591.5 27.1 reduce-scatter.15
  630.3 82.8 reduce-scatter.17
  716.6 66.3 reduce-scatter.25
  786.5 65.4 reduce-scatter.21
  855.4 65.4 reduce-scatter.23
  923.7 19.5 reduce-scatter.19
  945.5 27.5 reduce-scatter.27
